TPU v7x, 128 devices: a whole 4x4x4 slice. The times are simulated.
128 devices in a mesh: ep: 8 (over z_lo, x), fsdp: 16 (over z_hi, y, core).
Axes of the slice: x: 4, y: 4, z: 4 (z_hi: 2, z_lo: 2; z = z_hi * 2 + z_lo), core: 2. Of those that a mesh axis runs over, the one named last changes fastest.
Arguments:
- train_gate: float32 [64, 2048, 1408], P('ep', 'fsdp'), may hold values from -0.1875 to 0.1875
- other_gate: bfloat16 [64, 2048, 1408], P('ep', 'fsdp'), may hold values from -0.0625 to 0.0625
- train_up: float32 [64, 2048, 1408], P('ep', 'fsdp'), may hold values from -0.1875 to 0.1875
- other_up: bfloat16 [64, 2048, 1408], P('ep', 'fsdp'), may hold values from -0.0625 to 0.0625
- router_weight: float32 [2048, 64], P('fsdp', 'ep'), may hold values from -0.125 to 0.125
- router_gain: float32 [2048], P('fsdp'), may hold values from 0.25 to 1.75
Outputs:
- ready_gate: bfloat16 [64, 2048, 1408], P('ep', None, 'fsdp')
- ready_up: bfloat16 [64, 2048, 1408], P('ep', None, 'fsdp')
- scale_gate: float32 [64, 1408], P('ep', 'fsdp')
- scale_up: float32 [64, 1408], P('ep', 'fsdp')
- serve_router: bfloat16 [2048, 64], replicated
All inputs are finite; a program needn't handle non-finite values. Where the computation divides by a largest or mean magnitude, that divisor is 1e-20 or more.
Results may differ from a plain program's by a relative error of at most 0.001.
Values may be sent and summed in bfloat16 or wider, within the bound.
A program may use at most 128 MiB of HBM per device.

v0:
```python
import jax
import jax.numpy as jnp
from jax import lax
from jax.sharding import Mesh
from jax.sharding import PartitionSpec as P

EP = ("ep_0", "ep_1")


def sent_to_all(array, axis):
    peers = lax.axis_size(axis)
    return lax.all_to_all(
        jnp.broadcast_to(array[None], (peers, *array.shape)), axis, 0, 0, tiled=True
    )


def taken_together(array, axis):
    everything = sent_to_all(array, axis)
    return jnp.max(everything, axis=0)


def in_one(arrays, axis):
    flat, at, finished = (jnp.concatenate([a.reshape(-1) for a in arrays]), 0, [])
    total = taken_together(flat, axis)
    for a in arrays:
        finished.append(total[at : at + a.size].reshape(a.shape))
        at += a.size
    return tuple(finished)


def side_by_side(arrays, axis, split_dim, concat_dim, along):
    widths = [a.shape[along] for a in arrays]
    both = jnp.concatenate(arrays, axis=along)
    filled = lax.all_to_all(both, axis, split_axis=split_dim, concat_axis=concat_dim, tiled=True)
    return tuple(jnp.split(filled, [sum(widths[:k]) for k in range(1, len(widths))], axis=along))


def joined_along(parts, dim):
    lengths = list(parts.shape[1:])
    lengths[dim] *= parts.shape[0]
    return jnp.moveaxis(parts, 0, dim).reshape(lengths)


def gathered_copies(array, axis, dim):
    parts = sent_to_all(array, axis)
    return joined_along(parts, dim)


def stacked_from(array, axes, order):
    parts = array[None]
    for k in order:
        parts = lax.all_gather(parts, axes[k], axis=0, tiled=True)
    carried = [lax.axis_size(axes[k]) for k in reversed(order)]
    parts = parts.reshape(*carried, *array.shape)
    turned = sorted(range(len(order)), key=lambda place: order[len(order) - 1 - place])
    return parts.transpose(*turned, *range(len(order), parts.ndim)).reshape(-1, *array.shape)


def gather_axes(array, axes, order, dim):
    return joined_along(stacked_from(array, axes, order), dim)


def per_device(train_gate, other_gate, train_up, other_up, router_weight, router_gain):
    latest_gate = train_gate + other_gate.astype(jnp.float32)
    latest_up = train_up + other_up.astype(jnp.float32)
    scale_gate, scale_up = in_one(
        (jnp.max(jnp.abs(latest_gate), axis=1), jnp.max(jnp.abs(latest_up), axis=1)), "fsdp"
    )
    narrow_gate, narrow_up = (
        (latest_gate / jnp.expand_dims(scale_gate, 1)).astype(jnp.bfloat16),
        (latest_up / jnp.expand_dims(scale_up, 1)).astype(jnp.bfloat16),
    )
    ready_gate, ready_up = side_by_side((narrow_gate, narrow_up), "fsdp", 2, 1, 0)
    scale_gate = lax.dynamic_slice_in_dim(
        scale_gate, lax.axis_index("fsdp") * ready_gate.shape[2], ready_gate.shape[2], axis=1
    )
    scale_up = lax.dynamic_slice_in_dim(
        scale_up, lax.axis_index("fsdp") * ready_up.shape[2], ready_up.shape[2], axis=1
    )
    part_router = (router_weight * router_gain[:, None]).astype(jnp.bfloat16)
    row_router = gathered_copies(part_router, "fsdp", 0)
    serve_router = gather_axes(row_router, EP, (0, 1), 1)
    return (ready_gate, ready_up, scale_gate, scale_up, serve_router)


def solution(mesh):
    split = Mesh(mesh.devices.reshape(2, 4, mesh.shape["fsdp"]), ("ep_0", "ep_1", "fsdp"))
    return jax.shard_map(
        per_device,
        mesh=split,
        in_specs=(
            P(EP, "fsdp", None),
            P(EP, "fsdp", None),
            P(EP, "fsdp", None),
            P(EP, "fsdp", None),
            P("fsdp", EP),
            P("fsdp"),
        ),
        out_specs=(P(EP, None, "fsdp"), P(EP, None, "fsdp"), P(EP, "fsdp"), P(EP, "fsdp"), P()),
        check_vma=False,
    )
```

profile of v0, /device:TPU:8, one launch (start us, length us, event | category | flops | bytes accessed | tf_op | source)
XLA Modules:
  0.0 182.9 jit_solution(4989648456742953288)
XLA Ops:
  0.6 6.5 %copy.69 = f32[8,128,1408]{1,0,2:T(8,128)} copy(f32[8,128,1408]{2,1,0:T(8,128)} %param.6) | data formatting | bytes 11534336 | tf_op args[0]
  7.1 4.1 %copy.68 = bf16[8,128,1408]{1,0,2:T(8,128)(2,1)S(1)} copy(bf16[8,128,1408]{2,1,0:T(8,128)(2,1)} %param.7) | data formatting | bytes 5767168 | tf_op args[1]
  11.2 5.1 %abs_reduce_fusion.1 = f32[8,1408]{0,1:T(8,128)} fusion(f32[8,128,1408]{1,0,2:T(8,128)} %copy.69, bf16[8,128,1408]{1,0,2:T(8,128)(2,1)S(1)} %copy.68), kind=kLoop, calls=%fused_computation.5 | loop fusion | flops 5755904 | bytes 8695808 | tf_op jit(solution)/shard_map/reduce_max | solution.py:67
  16.3 1.3 copy.70
  17.6 6.5 %copy.72 = f32[8,128,1408]{1,0,2:T(8,128)} copy(f32[8,128,1408]{2,1,0:T(8,128)} %param.8) | data formatting | bytes 11534336 | tf_op args[2]
  24.1 4.9 %copy.71 = bf16[8,128,1408]{1,0,2:T(8,128)(2,1)} copy(bf16[8,128,1408]{2,1,0:T(8,128)(2,1)} %param.9) | data formatting | bytes 5767168 | tf_op args[3]
  29.0 5.6 %abs_reduce_fusion = f32[8,1408]{0,1:T(8,128)} fusion(f32[8,128,1408]{1,0,2:T(8,128)} %copy.72, bf16[8,128,1408]{1,0,2:T(8,128)(2,1)} %copy.71), kind=kLoop, calls=%fused_computation.3 | loop fusion | flops 5755904 | bytes 8695808 | tf_op jit(solution)/shard_map/reduce_max | solution.py:67
  34.6 1.3 copy.73
  35.9 1.8 %broadcast_in_dim.4 = f32[16,1,22528]{2,1,0:T(1,128)} broadcast(f32[22528]{0:T(1024)S(1)} %pad_maximum_fusion.1), dimensions={2} | broadcast | bytes 1531904 | tf_op jit(solution)/shard_map/broadcast_in_dim | solution.py:13
  37.8 8.2 %all-to-all-start = ((f32[16,1,22528]{2,1,0:T(1,128)}), f32[16,1,22528]{2,1,0:T(1,128)}, u32[]{:S(2)}, u32[]{:S(2)}) async-start(f32[16,1,22528]{2,1,0:T(1,128)} %broadcast_in_dim.4), calls=%async_computation | async-start | bytes 2883584 | tf_op jit(solution)/shard_map/all_to_all | solution.py:12
  46.1 19.1 %all-to-all-done = f32[16,1,22528]{2,1,0:T(1,128)} async-done(((f32[16,1,22528]{2,1,0:T(1,128)}), f32[16,1,22528]{2,1,0:T(1,128)}, u32[]{:S(2)}, u32[]{:S(2)}) %all-to-all-start) | async-done | bytes 1441824 | tf_op jit(solution)/shard_map/all_to_all | solution.py:12
  65.8 6.5 %all-to-all-start.2 = ((bf16[16,128,8]{1,2,0:T(8,128)(2,1)}), bf16[16,128,8]{1,2,0:T(8,128)(2,1)S(1)}, u32[]{:S(2)}, u32[]{:S(2)}) async-start(bf16[16,128,8]{1,2,0:T(8,128)(2,1)} %broadcast_in_dim.5), calls=%async_computation.2 | async-start | bytes 65536 | tf_op jit(solution)/shard_map/all_to_all | solution.py:12
  72.3 2.3 %reduce_max.29 = f32[22528]{0:T(1024)S(1)} reduce(f32[16,1,22528]{2,1,0:T(1,128)} %all-to-all-done, f32[]{:T(128)} %constant.5.clone.1), dimensions={0,1}, to_apply=%region_2.0 | reduce | flops 337920 | bytes 1531908 | tf_op jit(solution)/shard_map/reduce_max | solution.py:19
  74.6 1.1 copy.75
  75.7 1.1 copy.76
  76.9 6.8 %divide_convert_fusion = (bf16[8,128,1408]{1,0,2:T(8,128)(2,1)S(1)}, bf16[8,128,1408]{1,0,2:T(8,128)(2,1)S(1)}) fusion(f32[8,128,1408]{1,0,2:T(8,128)} %copy.72, bf16[8,128,1408]{1,0,2:T(8,128)(2,1)} %copy.71, f32[8,1408]{0,1:T(8,128)} %copy.76, f32[8,1408]{0,1:T(8,128)} %copy.75, f32[8,128,1408]{1,0,2:T(8,128)} %copy.69, bf16[8,128,1408]{1,0,2:T(8,128)(2,1)S(1)} %copy.68), kind=kLoop, calls=%fused_computation.1 | loop fusion | flops 11534336 | bytes 23158784 | tf_op jit(solution)/shard_map/convert_element_type | solution.py:71
  83.7 3.2 %pad_maximum_fusion = bf16[16,128,1408]{1,0,2:T(8,128)(2,1)} fusion(bf16[8,128,1408]{1,0,2:T(8,128)(2,1)S(1)} %get-tuple-element.9, bf16[8,128,1408]{1,0,2:T(8,128)(2,1)S(1)} %get-tuple-element.10), kind=kLoop, calls=%fused_computation | loop fusion | flops 11534336 | bytes 11534336 | tf_op jit(solution)/shard_map/concatenate | solution.py:33
  86.9 7.3 %all-to-all-start.1 = ((bf16[16,128,1408]{1,0,2:T(8,128)(2,1)}), bf16[16,128,1408]{1,0,2:T(8,128)(2,1)}, u32[]{:S(2)}, u32[]{:S(2)}) async-start(bf16[16,128,1408]{1,0,2:T(8,128)(2,1)} %pad_maximum_fusion), calls=%async_computation.1 | async-start | bytes 11534336 | tf_op jit(solution)/shard_map/all_to_all | solution.py:34
  94.2 64.7 %all_gather.6 = bf16[2,2048,8]{1,2,0:T(8,128)(2,1)S(1)} all-gather(bf16[1,2048,8]{1,2,0:T(8,128)(2,1)S(1)} %bitcast.27), channel_id=1, replica_groups=mesh['ep_0'=2,'ep_1'=4,'fsdp'=16] {'ep_0'}, dimensions={0}, use_global_device_ids=true | all-gather | bytes 98304 | tf_op jit(solution)/shard_map/all_gather | solution.py:52
  158.9 12.8 %all_gather.7 = bf16[8,2048,8]{1,2,0:T(8,128)(2,1)S(1)} all-gather(bf16[2,2048,8]{1,2,0:T(8,128)(2,1)S(1)} %all_gather.6), channel_id=1, replica_groups=mesh['ep_0'=2,'ep_1'=4,'fsdp'=16] {'ep_1'}, dimensions={0}, use_global_device_ids=true | all-gather | bytes 327680 | tf_op jit(solution)/shard_map/all_gather | solution.py:52
  173.1 4.1 %copy.77 = bf16[16,128,1408]{1,2,0:T(8,128)(2,1)S(1)} copy(bf16[16,128,1408]{1,0,2:T(8,128)(2,1)} %all-to-all-done.1) | data formatting | bytes 11534336 | tf_op jit(solution)/shard_map/all_to_all | solution.py:34
  177.2 1.0 slice_bitcast_fusion
  178.2 2.4 %copy.88 = bf16[8,16,11,8,128]{4,3,1,2,0:T(8,128)(2,1)} copy(bf16[8,16,11,8,128]{4,3,2,1,0:T(8,128)(2,1)S(1)} %get-tuple-element.5) | data formatting | bytes 5767168 | tf_op jit(solution)/shard_map/split | solution.py:35
  180.6 2.4 %copy.89 = bf16[8,16,11,8,128]{4,3,1,2,0:T(8,128)(2,1)} copy(bf16[8,16,11,8,128]{4,3,2,1,0:T(8,128)(2,1)S(1)} %get-tuple-element.6) | data formatting | bytes 5767168 | tf_op jit(solution)/shard_map/split | solution.py:35
  (16 shorter events, 2.1 us)
Async XLA Ops:
  29.0 17.0 %copy-start = (f32[128,8]{0,1:T(8,128)S(1)}, f32[128,8]{0,1:T(8,128)}, u32[]{:S(2)}) copy-start(f32[128,8]{0,1:T(8,128)} %param.10) | copy-start | bytes 12292
  29.0 17.0 %copy-start.1 = (f32[128]{0:T(128)S(1)}, f32[128]{0:T(128)}, u32[]{:S(2)}) copy-start(f32[128]{0:T(128)} %param.11) | copy-start | bytes 1540
  37.8 27.4 %all-to-all-start = ((f32[16,1,22528]{2,1,0:T(1,128)}), f32[16,1,22528]{2,1,0:T(1,128)}, u32[]{:S(2)}, u32[]{:S(2)}) async-start(f32[16,1,22528]{2,1,0:T(1,128)} %broadcast_in_dim.4), calls=%async_computation | async-start | bytes 2883584 | tf_op jit(solution)/shard_map/all_to_all | solution.py:12
  65.8 21.1 %all-to-all-start.2 = ((bf16[16,128,8]{1,2,0:T(8,128)(2,1)}), bf16[16,128,8]{1,2,0:T(8,128)(2,1)S(1)}, u32[]{:S(2)}, u32[]{:S(2)}) async-start(bf16[16,128,8]{1,2,0:T(8,128)(2,1)} %broadcast_in_dim.5), calls=%async_computation.2 | async-start | bytes 65536 | tf_op jit(solution)/shard_map/all_to_all | solution.py:12
  86.9 86.1 %all-to-all-start.1 = ((bf16[16,128,1408]{1,0,2:T(8,128)(2,1)}), bf16[16,128,1408]{1,0,2:T(8,128)(2,1)}, u32[]{:S(2)}, u32[]{:S(2)}) async-start(bf16[16,128,1408]{1,0,2:T(8,128)(2,1)} %pad_maximum_fusion), calls=%async_computation.1 | async-start | bytes 11534336 | tf_op jit(solution)/shard_map/all_to_all | solution.py:34
where the time goes:
time: 184 us; the launch traced here: 183 us
  blocking collectives  77.5 us (42%)
  local copies, waits for them, and re-layouts  40.6 us (22%)
  other arithmetic  23 us (12%)
  starting transfers between devices  22 us (12%)
  waiting for transfers between devices  19.2 us (10%)
    all_gather x2, blocking collectives, stacked_from(): parts = lax.all_gather(parts, axes[k], axis=0, tiled=True)  77.5 us
    unnamed x9, local copies, waits for them, and re-layouts  22.9 us
    all_to_all x2, waiting for transfers between devices, sent_to_all(): lax.all_to_all(jnp.broadcast_to(array[None], (peers, *array.shape)), axis...  19.2 us
    all_to_all x2, starting transfers between devices, sent_to_all(): lax.all_to_all(jnp.broadcast_to(array[None], (peers, *array.shape)), axis...  14.7 us
    all_to_all x1, starting transfers between devices, side_by_side(): lax.all_to_all(both, axis, split_axis=split_dim, concat_axis=concat_dim,...  7.29 us
    convert_element_type x1, other arithmetic, per_device(): (latest_up / jnp.expand_dims(scale_up, 1)).astype(jnp.bfloat16)  6.79 us
    reduce_max x1, other arithmetic, per_device(): jnp.max(jnp.abs(latest_up), axis=1)  5.58 us
    reduce_max x1, other arithmetic, per_device(): jnp.max(jnp.abs(latest_gate), axis=1)  5.11 us
  transfers between devices with their start and end apart: 3, of which 1 were waited for; matrix products, arithmetic and copies ran while one was open for 9% of the time, Pallas kernels for 0%

commit v1 on v0

--- a/solution.py
+++ b/solution.py
@@ -49,7 +49,9 @@
 def stacked_from(array, axes, order):
     parts = array[None]
     for k in order:
-        parts = lax.all_gather(parts, axes[k], axis=0, tiled=True)
+        parts = jnp.concatenate(
+            lax.all_to_all(jnp.stack([parts] * lax.axis_size(axes[k])), axes[k], 0, 0), axis=0
+        )
     carried = [lax.axis_size(axes[k]) for k in reversed(order)]
     parts = parts.reshape(*carried, *array.shape)
     turned = sorted(range(len(order)), key=lambda place: order[len(order) - 1 - place])

time: 184 us -> 194 us (1.054)
  waiting for transfers between devices: 19.2 us -> 80.5 us
  blocking collectives: 77.5 us -> 26.1 us
    all_gather x2 -> x0, blocking collectives: 77.5 us -> none  [stacked_from(): parts = lax.all_gather(parts, axes[k], axis=0, tiled=True)]
    all_to_all x1, waiting for transfers between devices: 0.01 us -> 76.4 us  [side_by_side(): lax.all_to_all(both, axis, split_axis=split_dim, concat_axis=concat_dim,...]
    all_to_all x0 -> x1, blocking collectives: none -> 26.1 us  [sent_to_all(): lax.all_to_all(jnp.broadcast_to(array[None], (peers, *array.shape)), axis...]
    all_to_all x2 -> x1, waiting for transfers between devices: 19.2 us -> 0.01 us  [sent_to_all(): lax.all_to_all(jnp.broadcast_to(array[None], (peers, *array.shape)), axis...]
    all_to_all x0 -> x2, starting transfers between devices: none -> 7.59 us  [stacked_from(): lax.all_to_all(jnp.stack([parts] * lax.axis_size(axes[k])), axes[k], 0, 0)]
    all_to_all x2 -> x1, starting transfers between devices: 14.7 us -> 8.24 us  [sent_to_all(): lax.all_to_all(jnp.broadcast_to(array[None], (peers, *array.shape)), axis...]
    all_to_all x0 -> x2, waiting for transfers between devices: none -> 4.09 us  [stacked_from(): lax.all_to_all(jnp.stack([parts] * lax.axis_size(axes[k])), axes[k], 0, 0)]
    reduce_max x1, other arithmetic: 5.58 us -> 3.32 us  [per_device(): jnp.max(jnp.abs(latest_up), axis=1)]
  transfers between devices with their start and end apart: 3 -> 4, of which waited for: 1 -> 2; matrix products, arithmetic and copies ran while one was open for 9% -> 26% of each run, Pallas kernels for 0% -> 0%
where the time goes in v1:
time: 194 us; the launch traced here: 193 us
  waiting for transfers between devices  80.5 us (41%)
  local copies, waits for them, and re-layouts  39.9 us (21%)
  blocking collectives  26.1 us (13%)
  starting transfers between devices  23.2 us (12%)
  other arithmetic  22.7 us (12%)
    all_to_all x1, waiting for transfers between devices, side_by_side(): lax.all_to_all(both, axis, split_axis=split_dim, concat_axis=concat_dim,...  76.4 us
    all_to_all x1, blocking collectives, sent_to_all(): lax.all_to_all(jnp.broadcast_to(array[None], (peers, *array.shape)), axis...  26.1 us
    unnamed x15, local copies, waits for them, and re-layouts  22.4 us
    all_to_all x1, starting transfers between devices, sent_to_all(): lax.all_to_all(jnp.broadcast_to(array[None], (peers, *array.shape)), axis...  8.24 us
    all_to_all x2, starting transfers between devices, stacked_from(): lax.all_to_all(jnp.stack([parts] * lax.axis_size(axes[k])), axes[k], 0, 0)  7.59 us
    all_to_all x1, starting transfers between devices, side_by_side(): lax.all_to_all(both, axis, split_axis=split_dim, concat_axis=concat_dim,...  7.4 us
    convert_element_type x1, other arithmetic, per_device(): (latest_up / jnp.expand_dims(scale_up, 1)).astype(jnp.bfloat16)  6.8 us
    reduce_max x1, other arithmetic, per_device(): jnp.max(jnp.abs(latest_gate), axis=1)  5.75 us
  transfers between devices with their start and end apart: 4, of which 2 were waited for; matrix products, arithmetic and copies ran while one was open for 26% of the time, Pallas kernels for 0%

profile of v1, /device:TPU:8, one launch (start us, length us, event | category | flops | bytes accessed | tf_op | source)
XLA Modules:
  0.0 193.1 jit_solution(18240230069763889969)
XLA Ops:
  1.9 8.2 %all-to-all-start.2 = ((bf16[16,128,8]{1,2,0:T(8,128)(2,1)}), bf16[16,128,8]{1,2,0:T(8,128)(2,1)S(1)}, u32[]{:S(2)}, u32[]{:S(2)}) async-start(bf16[16,128,8]{1,2,0:T(8,128)(2,1)} %broadcast_in_dim.5), calls=%async_computation.2 | async-start | bytes 65536 | tf_op jit(solution)/shard_map/all_to_all | solution.py:12
  10.2 6.6 %copy.76 = f32[8,128,1408]{1,0,2:T(8,128)} copy(f32[8,128,1408]{2,1,0:T(8,128)} %param.6) | data formatting | bytes 11534336 | tf_op args[0]
  16.8 3.4 %copy.75 = bf16[8,128,1408]{1,0,2:T(8,128)(2,1)} copy(bf16[8,128,1408]{2,1,0:T(8,128)(2,1)S(1)} %copy-done.2) | data formatting | bytes 5767168 | tf_op args[1]
  20.2 6.4 %copy.79 = f32[8,128,1408]{1,0,2:T(8,128)} copy(f32[8,128,1408]{2,1,0:T(8,128)} %param.8) | data formatting | bytes 11534336 | tf_op args[2]
  26.6 5.0 %copy.78 = bf16[8,128,1408]{1,0,2:T(8,128)(2,1)} copy(bf16[8,128,1408]{2,1,0:T(8,128)(2,1)} %param.9) | data formatting | bytes 5767168 | tf_op args[3]
  31.6 5.7 %abs_reduce_fusion.1 = f32[8,1408]{0,1:T(8,128)} fusion(f32[8,128,1408]{1,0,2:T(8,128)} %copy.76, bf16[8,128,1408]{1,0,2:T(8,128)(2,1)} %copy.75), kind=kLoop, calls=%fused_computation.5 | loop fusion | flops 5755904 | bytes 8695808 | tf_op jit(solution)/shard_map/reduce_max | solution.py:69
  37.3 3.3 %abs_reduce_fusion = f32[8,1408]{0,1:T(8,128)} fusion(f32[8,128,1408]{1,0,2:T(8,128)S(1)} %bitcast.23, bf16[8,128,1408]{1,0,2:T(8,128)(2,1)S(1)} %copy-done.1), kind=kLoop, calls=%fused_computation.3 | loop fusion | flops 5755904 | bytes 8695808 | tf_op jit(solution)/shard_map/reduce_max | solution.py:69
  40.7 1.5 copy.77
  42.1 1.3 copy.80
  44.2 3.3 %all-to-all-start.3 = ((bf16[2,1,2048,8]{2,3,1,0:T(8,128)(2,1)}), bf16[2,1,2048,8]{2,3,1,0:T(8,128)(2,1)S(1)}, u32[]{:S(2)}, u32[]{:S(2)}) async-start(bf16[2,1,2048,8]{2,3,1,0:T(8,128)(2,1)} %pad_maximum_fusion.2), calls=%async_computation.3 | async-start | bytes 131072 | tf_op jit(solution)/shard_map/all_to_all | solution.py:53
  47.5 4.1 %all-to-all-done.3 = bf16[2,1,2048,8]{2,3,1,0:T(8,128)(2,1)S(1)} async-done(((bf16[2,1,2048,8]{2,3,1,0:T(8,128)(2,1)}), bf16[2,1,2048,8]{2,3,1,0:T(8,128)(2,1)S(1)}, u32[]{:S(2)}, u32[]{:S(2)}) %all-to-all-start.3) | async-done | bytes 65568 | tf_op jit(solution)/shard_map/all_to_all | solution.py:53
  52.3 26.1 %all_to_all.36 = f32[16,1,22528]{2,1,0:T(1,128)} all-to-all(f32[16,1,22528]{2,1,0:T(1,128)S(1)} %broadcast_in_dim.4), channel_id=1, replica_groups=mesh['ep_0'=2,'ep_1'=4,'fsdp'=16] {'fsdp'}, dimensions={0} | all-to-all | bytes 2883584 | tf_op jit(solution)/shard_map/all_to_all | solution.py:12
  79.1 4.3 %all-to-all-start.4 = ((bf16[4,2,2048,8]{2,3,1,0:T(8,128)(2,1)}), bf16[4,2,2048,8]{2,3,1,0:T(8,128)(2,1)S(1)}, u32[]{:S(2)}, u32[]{:S(2)}) async-start(bf16[4,2,2048,8]{2,3,1,0:T(8,128)(2,1)} %stack.7), calls=%async_computation.4 | async-start | bytes 524288 | tf_op jit(solution)/shard_map/all_to_all | solution.py:53
  83.4 2.3 %reduce_max.29 = f32[22528]{0:T(1024)S(1)} reduce(f32[16,1,22528]{2,1,0:T(1,128)} %all_to_all.36, f32[]{:T(128)} %constant.5.clone.1), dimensions={0,1}, to_apply=%region_2.0 | reduce | flops 337920 | bytes 1531908 | tf_op jit(solution)/shard_map/reduce_max | solution.py:19
  85.7 1.2 copy.82
  86.9 1.1 copy.83
  88.0 6.8 %divide_convert_fusion = (bf16[8,128,1408]{1,0,2:T(8,128)(2,1)S(1)}, bf16[8,128,1408]{1,0,2:T(8,128)(2,1)S(1)}) fusion(f32[8,128,1408]{1,0,2:T(8,128)} %copy.79, bf16[8,128,1408]{1,0,2:T(8,128)(2,1)} %copy.78, f32[8,1408]{0,1:T(8,128)} %copy.83, f32[8,1408]{0,1:T(8,128)} %copy.82, f32[8,128,1408]{1,0,2:T(8,128)} %copy.76, bf16[8,128,1408]{1,0,2:T(8,128)(2,1)S(1)} %copy-done), kind=kLoop, calls=%fused_computation.1 | loop fusion | flops 11534336 | bytes 23158784 | tf_op jit(solution)/shard_map/convert_element_type | solution.py:73
  94.8 3.2 %pad_maximum_fusion = bf16[16,128,1408]{1,0,2:T(8,128)(2,1)} fusion(bf16[8,128,1408]{1,0,2:T(8,128)(2,1)S(1)} %get-tuple-element.9, bf16[8,128,1408]{1,0,2:T(8,128)(2,1)S(1)} %get-tuple-element.10), kind=kLoop, calls=%fused_computation | loop fusion | flops 11534336 | bytes 11534336 | tf_op jit(solution)/shard_map/concatenate | solution.py:33
  98.0 7.4 %all-to-all-start.1 = ((bf16[16,128,1408]{1,0,2:T(8,128)(2,1)}), bf16[16,128,1408]{1,0,2:T(8,128)(2,1)}, u32[]{:S(2)}, u32[]{:S(2)}) async-start(bf16[16,128,1408]{1,0,2:T(8,128)(2,1)} %pad_maximum_fusion), calls=%async_computation.1 | async-start | bytes 11534336 | tf_op jit(solution)/shard_map/all_to_all | solution.py:34
  106.8 76.4 %all-to-all-done.1 = bf16[16,128,1408]{1,0,2:T(8,128)(2,1)} async-done(((bf16[16,128,1408]{1,0,2:T(8,128)(2,1)}), bf16[16,128,1408]{1,0,2:T(8,128)(2,1)}, u32[]{:S(2)}, u32[]{:S(2)}) %all-to-all-start.1) | async-done | bytes 5767200 | tf_op jit(solution)/shard_map/all_to_all | solution.py:34
  183.2 4.1 %copy.84 = bf16[16,128,1408]{1,2,0:T(8,128)(2,1)S(1)} copy(bf16[16,128,1408]{1,0,2:T(8,128)(2,1)} %all-to-all-done.1) | data formatting | bytes 11534336 | tf_op jit(solution)/shard_map/all_to_all | solution.py:34
  187.4 1.0 slice_bitcast_fusion
  188.4 2.4 %copy.95 = bf16[8,16,11,8,128]{4,3,1,2,0:T(8,128)(2,1)} copy(bf16[8,16,11,8,128]{4,3,2,1,0:T(8,128)(2,1)S(1)} %get-tuple-element.5) | data formatting | bytes 5767168 | tf_op jit(solution)/shard_map/split | solution.py:35
  190.7 2.4 %copy.96 = bf16[8,16,11,8,128]{4,3,1,2,0:T(8,128)(2,1)} copy(bf16[8,16,11,8,128]{4,3,2,1,0:T(8,128)(2,1)S(1)} %get-tuple-element.6) | data formatting | bytes 5767168 | tf_op jit(solution)/shard_map/split | solution.py:35
  (26 shorter events, 4.9 us)
Async XLA Ops:
  1.9 41.6 %all-to-all-start.2 = ((bf16[16,128,8]{1,2,0:T(8,128)(2,1)}), bf16[16,128,8]{1,2,0:T(8,128)(2,1)S(1)}, u32[]{:S(2)}, u32[]{:S(2)}) async-start(bf16[16,128,8]{1,2,0:T(8,128)(2,1)} %broadcast_in_dim.5), calls=%async_computation.2 | async-start | bytes 65536 | tf_op jit(solution)/shard_map/all_to_all | solution.py:12
  10.2 6.6 %copy-start.2 = (bf16[8,128,1408]{2,1,0:T(8,128)(2,1)S(1)}, bf16[8,128,1408]{2,1,0:T(8,128)(2,1)}, u32[]{:S(2)}) copy-start(bf16[8,128,1408]{2,1,0:T(8,128)(2,1)} %param.7) | copy-start | bytes 8650756
  26.6 10.7 %slice-start = ((s8[5767168]{0:T(1024)(128)(4,1)}), s8[1572864]{0:T(1024)(128)(4,1)S(1)}, s32[]{:S(2)}) async-start(s8[5767168]{0:T(1024)(128)(4,1)} %bitcast.22), calls=%async_computation.5 | async-start | bytes 3145728
  31.6 5.8 %slice-start.1 = ((s8[5767168]{0:T(1024)(128)(4,1)}), s8[4194304]{0:T(1024)(128)(4,1)S(1)}, s32[]{:S(2)}) async-start(s8[5767168]{0:T(1024)(128)(4,1)} %bitcast.22), calls=%async_computation.6 | async-start | bytes 8388608
  31.6 5.8 %copy-start.1 = (bf16[8,128,1408]{1,0,2:T(8,128)(2,1)S(1)}, bf16[8,128,1408]{1,0,2:T(8,128)(2,1)}, u32[]{:S(2)}) copy-start(bf16[8,128,1408]{1,0,2:T(8,128)(2,1)} %copy.78) | copy-start | bytes 8650756
  40.7 47.3 %copy-start = (bf16[8,128,1408]{1,0,2:T(8,128)(2,1)S(1)}, bf16[8,128,1408]{1,0,2:T(8,128)(2,1)}, u32[]{:S(2)}) copy-start(bf16[8,128,1408]{1,0,2:T(8,128)(2,1)} %copy.75) | copy-start | bytes 8650756
  44.2 7.4 %all-to-all-start.3 = ((bf16[2,1,2048,8]{2,3,1,0:T(8,128)(2,1)}), bf16[2,1,2048,8]{2,3,1,0:T(8,128)(2,1)S(1)}, u32[]{:S(2)}, u32[]{:S(2)}) async-start(bf16[2,1,2048,8]{2,3,1,0:T(8,128)(2,1)} %pad_maximum_fusion.2), calls=%async_computation.3 | async-start | bytes 131072 | tf_op jit(solution)/shard_map/all_to_all | solution.py:53
  79.1 18.9 %all-to-all-start.4 = ((bf16[4,2,2048,8]{2,3,1,0:T(8,128)(2,1)}), bf16[4,2,2048,8]{2,3,1,0:T(8,128)(2,1)S(1)}, u32[]{:S(2)}, u32[]{:S(2)}) async-start(bf16[4,2,2048,8]{2,3,1,0:T(8,128)(2,1)} %stack.7), calls=%async_computation.4 | async-start | bytes 524288 | tf_op jit(solution)/shard_map/all_to_all | solution.py:53
  98.0 85.2 %all-to-all-start.1 = ((bf16[16,128,1408]{1,0,2:T(8,128)(2,1)}), bf16[16,128,1408]{1,0,2:T(8,128)(2,1)}, u32[]{:S(2)}, u32[]{:S(2)}) async-start(bf16[16,128,1408]{1,0,2:T(8,128)(2,1)} %pad_maximum_fusion), calls=%async_computation.1 | async-start | bytes 11534336 | tf_op jit(solution)/shard_map/all_to_all | solution.py:34
